TPU v7x, 256 devices: a 2x2x32 block of a 4x8x32 slice. The times are simulated.
256 devices in a mesh: groups: 4 (over x, y), blk: 32 (over z), rows: 2 (over core).
Axes of the slice: x: 2, y: 2, z: 32, core: 2. Of those that a mesh axis runs over, the one named last changes fastest.
The devices are a block of a 4x8x32 slice.
Arguments:
- features: bfloat16 [16, 16, 1024, 512], P('groups', 'rows', 'blk'), parts along dimension 0, may hold values from -60 to 60
- gain_in: float32 [512], replicated, may hold values from 0.25 to 1.75
- shift_in: float32 [512], replicated, may hold values from -3 to 3
- conv_first: bfloat16 [3, 3, 512, 256], replicated, may hold values from -0.09375 to 0.09375
- bias_first: float32 [256], replicated, may hold values from -3 to 3
- short_weight: bfloat16 [512, 256], replicated, may hold values from -0.25 to 0.25
- short_bias: float32 [256], replicated, may hold values from -3 to 3
- gains_rest: float32 [5, 256], replicated, may hold values from 0.25 to 1.75
- shifts_rest: float32 [5, 256], replicated, may hold values from -3 to 3
- convs_rest: bfloat16 [5, 3, 3, 256, 256], replicated, may hold values from -0.125 to 0.125
- biases_rest: float32 [5, 256], replicated, may hold values from -3 to 3
Outputs:
- decoded: bfloat16 [16, 16, 1024, 256], P('groups', 'rows', 'blk'), parts along dimension 0
There are 4 independent parts, one for each index of `groups`. A program takes and returns all parts, laid end to end along the dimension named above; an argument that names none is the same for every part. Nothing has to cross between parts.
All inputs are finite; a program needn't handle non-finite values.
Results may differ from a plain program's by a relative error of at most 0.0065.
Values may be sent and summed in bfloat16 or wider, within the bound.
A program may use at most 128 MiB of HBM per device.

v0:
```python
import functools

import jax
import jax.numpy as jnp
from jax import lax
from jax.experimental import pallas as pl
from jax.experimental.pallas import tpu as pltpu
from jax.sharding import PartitionSpec as P

GROUPS = 32
RESNETS = 3
EPS = 1e-06
LANES = 128
MESH = pl.DeviceIdType.MESH
F32 = jnp.float32
BF16 = jnp.bfloat16


def iota(shape, dim):
    return lax.broadcasted_iota(jnp.int32, shape, dim)


def three_parts(values, part):
    high = values.astype(BF16)
    rest = values - high.astype(F32)
    middle = rest.astype(BF16)
    low = (rest - middle.astype(F32)).astype(BF16)
    picked = jnp.where(part == 0, high.astype(F32), jnp.where(part == 1, middle.astype(F32), low.astype(F32)))
    return jnp.where(part < 3, picked, 0.0).astype(BF16)


def kernel(
    nblk,
    nrow,
    halves,
    x_hbm,
    gain_in,
    shift_in,
    w1_hbm,
    bias_first,
    sw_hbm,
    short_bias,
    gains,
    shifts,
    wr_hbm,
    biases,
    out_hbm,
    xv,
    w1,
    wr,
    sw,
    v0,
    vs,
    stream,
    a1,
    a2,
    outv,
    col_s1,
    col_r1,
    row_r1,
    cor_s1,
    cor_r1,
    col_s2,
    col_r2,
    row_r2,
    cor_s2,
    cor_r2,
    stat_s,
    stat_r,
    x_sem,
    w_sem,
    out_sem,
    stat_ssem,
    stat_rsem,
    halo_ssem,
    colr_sem,
    rowr_sem,
    corr_sem,
):
    images, height, width, _ = xv.shape
    per = images // halves
    slots = 2 * per
    pixels = height * width
    z = lax.axis_index("blk")
    c = lax.axis_index("rows")
    oc = 1 - c
    right = lax.rem(z + 1, nblk)
    left = lax.rem(z + nblk - 1, nblk)
    me = z * nrow + c
    edge = (height - 1) * (1 - c)
    halo_row = (height + 1) * (1 - c)
    zero_row = (height + 1) * c

    x_copies = [pltpu.make_async_copy(x_hbm.at[i], xv.at[i], x_sem.at[i]) for i in range(images)]
    for copy in x_copies:
        copy.start()
    w_copies = [
        pltpu.make_async_copy(sw_hbm, sw, w_sem.at[0]),
        pltpu.make_async_copy(w1_hbm, w1, w_sem.at[1]),
    ] + [pltpu.make_async_copy(wr_hbm.at[i], wr.at[i], w_sem.at[2 + i]) for i in range(wr_hbm.shape[0])]
    for copy in w_copies:
        copy.start()

    barrier = pltpu.get_barrier_semaphore()

    def greet(d, carry):
        zz = lax.rem(z + d, nblk)
        pl.semaphore_signal(barrier, 1, device_id={"blk": zz, "rows": oc}, device_id_type=MESH)

        @pl.when(d > 0)
        def _():
            pl.semaphore_signal(barrier, 1, device_id={"blk": zz, "rows": c}, device_id_type=MESH)

        return carry

    lax.fori_loop(0, nblk, greet, 0)

    for a in (a1, a2):
        for i in range(images):
            a[i, zero_row] = jnp.zeros(a.shape[2:], BF16)

    def gather_matrix(channels):
        return (iota((channels, LANES), 0) // (channels // GROUPS) == iota((channels, LANES), 1) % GROUPS).astype(F32).astype(BF16)

    def spread_matrix(channels):
        return (iota((LANES, channels), 0) % GROUPS == iota((LANES, channels), 1) // (channels // GROUPS)).astype(F32).astype(BF16)

    def local_stats(k, h, rows):
        channels = rows[0].shape[1]
        which = iota((16, channels), 0)
        base = jnp.broadcast_to(rows[0], (16, channels))
        for j in range(1, slots):
            base = jnp.where(which % slots == j, rows[j], base)
        lhs = three_parts(base, which // slots)
        dots = jnp.dot(lhs, gather_matrix(channels), preferred_element_type=F32)
        slot_of_row = iota((16, LANES), 0) % slots
        slot_of_lane = iota((16, LANES), 1) // GROUPS
        packed = jnp.sum(jnp.where(slot_of_row == slot_of_lane, dots, 0.0), axis=0, keepdims=True)
        stat_s[k, h] = jnp.broadcast_to(packed, (8, LANES))
        stat_r[k, h, pl.ds(me, 1)] = packed

    def send_stats(k, h):
        source = stat_s.at[k, h, pl.ds(0, 1)]
        target = stat_r.at[k, h, pl.ds(me, 1)]

        def to(zz, cc):
            pltpu.make_async_remote_copy(
                source, target, stat_ssem.at[k, h], stat_rsem.at[k, h],
                device_id={"blk": zz, "rows": cc}, device_id_type=MESH,
            ).start()

        half_way = nblk // 2
        to(lax.rem(z + half_way, nblk), oc)
        to(lax.rem(z + half_way, nblk), c)

        def step(i, carry):
            d = half_way - 1 - i
            for zz in (lax.rem(z + d, nblk), lax.rem(z + nblk - d, nblk)):
                to(zz, oc)
                to(zz, c)
            return carry

        lax.fori_loop(0, half_way - 1, step, 0)
        to(z, oc)

    def wait_stats(k, h):
        count = nblk * nrow - 1
        copy = pltpu.make_async_remote_copy(
            stat_r.at[k, h, pl.ds(0, count)], stat_r.at[k, h, pl.ds(0, count)],
            stat_ssem.at[k, h], stat_rsem.at[k, h], device_id={"rows": oc}, device_id_type=MESH,
        )
        copy.wait_send()
        copy.wait_recv()

    def scales(k, h, channels, gain, shift):
        count = pixels * nblk * nrow * (channels // GROUPS)
        total = jnp.sum(stat_r[k, h], axis=0, keepdims=True) / count
        total = jnp.broadcast_to(total, (16, LANES))
        center = pltpu.roll(total, GROUPS, 1)
        spread = lax.rsqrt(jnp.maximum(total - center * center, 0.0) + EPS)
        slot_of_lane = iota((16, LANES), 1) // GROUPS
        stat = jnp.where(slot_of_lane % 2 == 1, spread, total)
        row = iota((16, LANES), 0)
        stat = jnp.where(slot_of_lane == row % slots, stat, 0.0)
        lhs = three_parts(stat, row // slots)
        dots = jnp.dot(lhs, spread_matrix(channels), preferred_element_type=F32)
        pick = lambda j: dots[j : j + 1] + dots[slots + j : slots + j + 1] + dots[2 * slots + j : 2 * slots + j + 1]
        result = []
        for i in range(per):
            a = pick(2 * i + 1) * gain
            result.append((0.5 * a, 0.5 * (shift - pick(2 * i) * a)))
        return result

    def activate(values, ab):
        half = values * ab[0] + ab[1]
        return half + half * jnp.tanh(half)

    class Halo:
        pass

    def halo_of(k):
        o = Halo()
        first = k == 0
        o.v = v0 if first else vs.at[k - 1]
        o.col_s = col_s1 if first else col_s2.at[k - 1]
        o.col_r = col_r1 if first else col_r2.at[k - 1]
        o.row_r = row_r1 if first else row_r2.at[k - 1]
        o.cor_s = cor_s1 if first else cor_s2.at[k - 1]
        o.cor_r = cor_r1 if first else cor_r2.at[k - 1]
        o.channels = o.v.shape[-1]
        return o

    def halo_copies(k, h):
        o = halo_of(k)
        copies = []
        for side, (near, blk) in enumerate(((0, right), (1, left))):
            copies.append(pltpu.make_async_remote_copy(
                o.col_s.at[h, side], o.col_r.at[h, side], halo_ssem.at[k, h, 2 * side], colr_sem.at[k, h, side],
                device_id={"blk": blk, "rows": c}, device_id_type=MESH))
            copies.append(pltpu.make_async_remote_copy(
                o.cor_s.at[h, side], o.cor_r.at[h, side], halo_ssem.at[k, h, 2 * side + 1], corr_sem.at[k, h, side],
                device_id={"blk": blk, "rows": oc}, device_id_type=MESH))
        copies.append(pltpu.make_async_remote_copy(
            o.v.at[pl.ds(h * per, per), pl.ds(edge * width, width)], o.row_r.at[h], halo_ssem.at[k, h, 4], rowr_sem.at[k, h],
            device_id={"rows": oc}, device_id_type=MESH))
        return copies

    def prepare_halo(k, h):
        o = halo_of(k)
        for side in range(2):
            q = width - 1 if side == 0 else 0
            cols = []
            corners = []
            for i in range(per):
                image = h * per + i
                which = iota((height, o.channels), 0)
                col = jnp.broadcast_to(o.v[image, pl.ds(q, 1), :], (height, o.channels))
                for r in range(1, height):
                    col = jnp.where(which == r, o.v[image, pl.ds(r * width + q, 1), :], col)
                cols.append(col)
                corners.append(o.v[image, pl.ds(edge * width + q, 1), :])
            o.col_s[h, side] = jnp.concatenate(cols, axis=0).astype(BF16)
            for i in range(per):
                o.cor_s[h, side, pl.ds(i, 1)] = corners[i]

    def emit(k, h, rows):
        local_stats(k, h, rows)
        send_stats(k, h)
        prepare_halo(k, h)
        for copy in halo_copies(k, h):
            copy.start()

    def load(k, h, a, gain, shift):
        o = halo_of(k)
        channels = o.channels
        wait_stats(k, h)
        factors = scales(k, h, channels, gain, shift)
        for copy in halo_copies(k, h):
            copy.wait()
        column = iota((width, channels), 0)

        def put(image, row, act, low, high):
            a[image, row, :, pl.ds(0, channels)] = jnp.where(column == 0, low, pltpu.roll(act, 1, 0)).astype(BF16)
            a[image, row, :, pl.ds(channels, channels)] = act.astype(BF16)
            a[image, row, :, pl.ds(2 * channels, channels)] = jnp.where(
                column == width - 1, high, pltpu.roll(act, width - 1, 0)).astype(BF16)

        for i in range(per):
            image = h * per + i
            ab = factors[i]
            sides = [activate(o.col_r[h, s, pl.ds(i * height, height)].astype(F32), ab) for s in range(2)]
            corner = [activate(o.cor_r[h, s, pl.ds(i, 1)], ab) for s in range(2)]
            for r in range(height):
                act = activate(o.v[image, pl.ds(r * width, width), :], ab)
                put(image, r + 1, act, sides[0][r : r + 1], sides[1][r : r + 1])
            act = activate(o.row_r[h, i], ab)
            put(image, halo_row, act, corner[0], corner[1])

    def convolve(a, image, weight):
        depth = a.shape[-1]
        total = None
        for d in range(3):
            lhs = a[image, d : d + height].reshape(pixels, depth)
            term = jnp.dot(lhs, weight[d].reshape(depth, weight.shape[-1]), preferred_element_type=F32)
            total = term if total is None else total + term
        return total

    def sums(values):
        return [jnp.sum(values, axis=0, keepdims=True), jnp.sum(values * values, axis=0, keepdims=True)]

    for h in range(halves):
        for i in range(per):
            x_copies[h * per + i].wait()
    rows0 = []
    for image in range(images):
        values = xv[image].reshape(pixels, xv.shape[-1]).astype(F32)
        v0[image] = values
        rows0.append(sums(values))
    pl.semaphore_wait(barrier, nblk * nrow - 1)
    for h in range(halves):
        emit(0, h, sum(rows0[h * per : (h + 1) * per], []))

    w_copies[0].wait()
    for image in range(images):
        stream[image] = jnp.dot(
            xv[image].reshape(pixels, xv.shape[-1]), sw[...], preferred_element_type=F32) + short_bias[...]

    last = 2 * RESNETS - 1
    for k in range(2 * RESNETS):
        if k == 0:
            a, gain, shift, weight, bias = a1, gain_in[...], shift_in[...], w1, bias_first[...]
        else:
            j = k - 1
            a, gain, shift, weight, bias = a2, gains[j : j + 1], shifts[j : j + 1], wr.at[j], biases[j : j + 1]
        for h in range(halves):
            load(k, h, a, gain, shift)
            if h == 0:
                w_copies[1 + k].wait()
            rows = []
            for i in range(per):
                image = h * per + i
                result = convolve(a, image, weight) + bias
                if k % 2 == 1:
                    result = result + stream[image]
                rounded = result.astype(BF16)
                if k == last:
                    outv[image] = rounded.reshape(height, width, rounded.shape[-1])
                else:
                    values = rounded.astype(F32)
                    vs[k, image] = values
                    if k % 2 == 1:
                        stream[image] = values
                    rows += sums(values)
            if k < last:
                emit(k + 1, h, rows)
            else:
                pltpu.make_async_copy(
                    outv.at[pl.ds(h * per, per)], out_hbm.at[pl.ds(h * per, per)], out_sem.at[h]).start()
    for h in range(halves):
        pltpu.make_async_copy(
            outv.at[pl.ds(h * per, per)], out_hbm.at[pl.ds(h * per, per)], out_sem.at[h]).wait()


def run(nblk, nrow, halves, *args):
    x = args[0]
    w1, wr = args[3], args[9]
    images, height, width, cin = x.shape
    ch = w1.shape[-1]
    per = images // halves
    stages = 2 * RESNETS
    anywhere = pl.BlockSpec(memory_space=pl.ANY)
    inside = pl.BlockSpec(memory_space=pltpu.VMEM)
    specs = [anywhere, inside, inside, anywhere, inside, anywhere, inside, inside, inside, anywhere, inside]
    fixed = list(args)
    for j in (1, 2, 4, 6):
        fixed[j] = args[j].reshape(1, -1)

    def halo_buffers(lead, channels):
        return [
            pltpu.VMEM((*lead, halves, 2, per * height, channels), BF16),
            pltpu.VMEM((*lead, halves, 2, per * height, channels), BF16),
            pltpu.VMEM((*lead, halves, per, width, channels), F32),
            pltpu.VMEM((*lead, halves, 2, 8, channels), F32),
            pltpu.VMEM((*lead, halves, 2, 8, channels), F32),
        ]

    return pl.pallas_call(
        functools.partial(kernel, nblk, nrow, halves),
        out_shape=jax.ShapeDtypeStruct((images, height, width, ch), BF16),
        in_specs=specs,
        out_specs=anywhere,
        scratch_shapes=[
            pltpu.VMEM(x.shape, BF16),
            pltpu.VMEM(w1.shape, BF16),
            pltpu.VMEM(wr.shape, BF16),
            pltpu.VMEM((cin, ch), BF16),
            pltpu.VMEM((images, height * width, cin), F32),
            pltpu.VMEM((stages - 1, images, height * width, ch), F32),
            pltpu.VMEM((images, height * width, ch), F32),
            pltpu.VMEM((images, height + 2, width, 3 * cin), BF16),
            pltpu.VMEM((images, height + 2, width, 3 * ch), BF16),
            pltpu.VMEM((images, height, width, ch), BF16),
            *halo_buffers((), cin),
            *halo_buffers((stages - 1,), ch),
            pltpu.VMEM((stages, halves, 8, LANES), F32),
            pltpu.VMEM((stages, halves, nblk * nrow, LANES), F32),
            pltpu.SemaphoreType.DMA((images,)),
            pltpu.SemaphoreType.DMA((1 + stages,)),
            pltpu.SemaphoreType.DMA((halves,)),
            pltpu.SemaphoreType.DMA((stages, halves)),
            pltpu.SemaphoreType.DMA((stages, halves)),
            pltpu.SemaphoreType.DMA((stages, halves, 5)),
            pltpu.SemaphoreType.DMA((stages, halves, 2)),
            pltpu.SemaphoreType.DMA((stages, halves)),
            pltpu.SemaphoreType.DMA((stages, halves, 2)),
        ],
        compiler_params=pltpu.CompilerParams(
            collective_id=0, has_side_effects=True, vmem_limit_bytes=60 * 1024 * 1024),
    )(*fixed)


def solution(mesh):
    placed = (P("groups", "rows", "blk", None),) + (P(),) * 10
    return jax.shard_map(
        functools.partial(run, mesh.shape["blk"], mesh.shape["rows"], 2),
        mesh=mesh,
        in_specs=placed,
        out_specs=P("groups", "rows", "blk", None),
        check_vma=False,
    )
```

profile of v0, /device:TPU:37, one launch (start us, length us, event | category | flops | bytes accessed | tf_op | source)
XLA Modules:
  0.0 120.7 jit_solution(5291092816658798385)
XLA Ops:
  0.0 118.8 %shard_map.109 = bf16[4,8,32,256]{3,2,1,0:T(8,128)(2,1)} custom-call(bf16[4,8,32,512]{3,2,1,0:T(8,128)(2,1)} %x_hbm.1, f32[1,512]{1,0:T(1,128)} %bitcast.4, f32[1,512]{1,0:T(1,128)} %bitcast.5, bf16[3,3,512,256]{3,2,1,0:T(8,128)(2,1)} %w1_hbm.1, f32[1,256]{1,0:T(1,128)} %bitcast.6, bf16[512,256]{1,0:T(8,128)(2,1)} %sw_hbm.1, f32[1,256]{1,0:T(1,128)} %bitcast.7, ...), custom_call_target="tpu_custom_call" | custom-call | tf_op jit(solution)/shard_map/pallas_call | solution.py:367
  118.8 1.9 %copy.13 = bf16[4,8,32,256]{3,2,1,0:T(8,128)(2,1)} copy(bf16[4,8,32,256]{3,2,1,0:T(8,128)(2,1)} %shard_map.109) | data formatting | bytes 1048576
where the time goes:
time: 121 us
  Pallas kernels  119 us (98%)
  local copies, waits for them, and re-layouts  1.87 us (2%)
    pallas_call x1, Pallas kernels, run(): pl.pallas_call(functools.partial(kernel, nblk, nrow, halves), out_shape=j...  119 us

commit v1 on v0

--- a/solution.py
+++ b/solution.py
@@ -29,22 +29,43 @@
     return jnp.where(part < 3, picked, 0.0).astype(BF16)
 
 
+def gather_matrix(channels):
+    shape = (channels, LANES)
+    return (iota(shape, 0) // (channels // GROUPS) == iota(shape, 1) % GROUPS).astype(F32).astype(BF16)
+
+
+def spread_matrix(channels):
+    shape = (LANES, channels)
+    return (iota(shape, 0) % GROUPS == iota(shape, 1) // (channels // GROUPS)).astype(F32).astype(BF16)
+
+
 def kernel(
     nblk,
     nrow,
     halves,
     x_hbm,
+    gain_in_hbm,
+    shift_in_hbm,
+    w1_hbm,
+    bias_first_hbm,
+    sw_hbm,
+    short_bias_hbm,
+    gains_hbm,
+    shifts_hbm,
+    wr_hbm,
+    biases_hbm,
+    outv,
     gain_in,
     shift_in,
-    w1_hbm,
     bias_first,
-    sw_hbm,
     short_bias,
     gains,
     shifts,
-    wr_hbm,
     biases,
-    out_hbm,
+    gather1,
+    gather2,
+    spread1,
+    spread2,
     xv,
     w1,
     wr,
@@ -54,7 +75,6 @@
     stream,
     a1,
     a2,
-    outv,
     col_s1,
     col_r1,
     row_r1,
@@ -67,9 +87,13 @@
     cor_r2,
     stat_s,
     stat_r,
+    relay_s,
+    relay_r,
     x_sem,
     w_sem,
-    out_sem,
+    p_sem,
+    relay_ssem,
+    relay_rsem,
     stat_ssem,
     stat_rsem,
     halo_ssem,
@@ -91,39 +115,46 @@
     halo_row = (height + 1) * (1 - c)
     zero_row = (height + 1) * c
 
+    half_way = nblk // 2
+    reach = half_way // 2
+    far_from = 2 * half_way // 3 + 1
+
+    def at(offset):
+        return lax.rem(z + nblk + offset, nblk)
+
+    barrier = pltpu.get_barrier_semaphore()
+
+    def greet(i, carry):
+        d = reach - i
+        for zz in (at(d), at(-d)):
+            for cc in (c, oc):
+                pl.semaphore_signal(barrier, 1, device_id={"blk": zz, "rows": cc}, device_id_type=MESH)
+        return carry
+
+    lax.fori_loop(0, reach, greet, 0)
+    pl.semaphore_signal(barrier, 1, device_id={"rows": oc}, device_id_type=MESH)
+
     x_copies = [pltpu.make_async_copy(x_hbm.at[i], xv.at[i], x_sem.at[i]) for i in range(images)]
-    for copy in x_copies:
-        copy.start()
     w_copies = [
         pltpu.make_async_copy(sw_hbm, sw, w_sem.at[0]),
         pltpu.make_async_copy(w1_hbm, w1, w_sem.at[1]),
     ] + [pltpu.make_async_copy(wr_hbm.at[i], wr.at[i], w_sem.at[2 + i]) for i in range(wr_hbm.shape[0])]
-    for copy in w_copies:
+    p_copies = [
+        pltpu.make_async_copy(source, target, p_sem.at[i])
+        for i, (source, target) in enumerate((
+            (gain_in_hbm, gain_in), (shift_in_hbm, shift_in), (bias_first_hbm, bias_first), (short_bias_hbm, short_bias),
+            (gains_hbm, gains), (shifts_hbm, shifts), (biases_hbm, biases)))
+    ]
+    for copy in x_copies + p_copies + w_copies:
         copy.start()
 
-    barrier = pltpu.get_barrier_semaphore()
-
-    def greet(d, carry):
-        zz = lax.rem(z + d, nblk)
-        pl.semaphore_signal(barrier, 1, device_id={"blk": zz, "rows": oc}, device_id_type=MESH)
-
-        @pl.when(d > 0)
-        def _():
-            pl.semaphore_signal(barrier, 1, device_id={"blk": zz, "rows": c}, device_id_type=MESH)
-
-        return carry
-
-    lax.fori_loop(0, nblk, greet, 0)
-
+    gather1[...] = gather_matrix(gather1.shape[0])
+    gather2[...] = gather_matrix(gather2.shape[0])
+    spread1[...] = spread_matrix(spread1.shape[1])
+    spread2[...] = spread_matrix(spread2.shape[1])
     for a in (a1, a2):
         for i in range(images):
             a[i, zero_row] = jnp.zeros(a.shape[2:], BF16)
-
-    def gather_matrix(channels):
-        return (iota((channels, LANES), 0) // (channels // GROUPS) == iota((channels, LANES), 1) % GROUPS).astype(F32).astype(BF16)
-
-    def spread_matrix(channels):
-        return (iota((LANES, channels), 0) % GROUPS == iota((LANES, channels), 1) // (channels // GROUPS)).astype(F32).astype(BF16)
 
     def local_stats(k, h, rows):
         channels = rows[0].shape[1]
@@ -132,39 +163,42 @@
         for j in range(1, slots):
             base = jnp.where(which % slots == j, rows[j], base)
         lhs = three_parts(base, which // slots)
-        dots = jnp.dot(lhs, gather_matrix(channels), preferred_element_type=F32)
+        dots = jnp.dot(lhs, (gather1 if k == 0 else gather2)[...], preferred_element_type=F32)
         slot_of_row = iota((16, LANES), 0) % slots
         slot_of_lane = iota((16, LANES), 1) // GROUPS
         packed = jnp.sum(jnp.where(slot_of_row == slot_of_lane, dots, 0.0), axis=0, keepdims=True)
         stat_s[k, h] = jnp.broadcast_to(packed, (8, LANES))
         stat_r[k, h, pl.ds(me, 1)] = packed
 
-    def send_stats(k, h):
-        source = stat_s.at[k, h, pl.ds(0, 1)]
-        target = stat_r.at[k, h, pl.ds(me, 1)]
-
-        def to(zz, cc):
-            pltpu.make_async_remote_copy(
-                source, target, stat_ssem.at[k, h], stat_rsem.at[k, h],
-                device_id={"blk": zz, "rows": cc}, device_id_type=MESH,
-            ).start()
-
-        half_way = nblk // 2
-        to(lax.rem(z + half_way, nblk), oc)
-        to(lax.rem(z + half_way, nblk), c)
-
+    def stat_to(k, h, zz, cc):
+        pltpu.make_async_remote_copy(
+            stat_s.at[k, h, pl.ds(0, 1)], stat_r.at[k, h, pl.ds(me, 1)], stat_ssem.at[k, h], stat_rsem.at[k, h],
+            device_id={"blk": zz, "rows": cc}, device_id_type=MESH,
+        ).start()
+
+    def send_between(k, hs, high, low):
         def step(i, carry):
-            d = half_way - 1 - i
-            for zz in (lax.rem(z + d, nblk), lax.rem(z + nblk - d, nblk)):
-                to(zz, oc)
-                to(zz, c)
+            d = high - i
+            for zz in (at(d), at(-d)):
+                for h in hs:
+                    stat_to(k, h, zz, oc)
+                    stat_to(k, h, zz, c)
             return carry
 
-        lax.fori_loop(0, half_way - 1, step, 0)
-        to(z, oc)
+        if high >= low:
+            lax.fori_loop(0, high - low + 1, step, 0)
+
+    def send_far(k, h):
+        stat_to(k, h, at(half_way), oc)
+        stat_to(k, h, at(half_way), c)
+        send_between(k, (h,), half_way - 1, far_from)
+
+    def send_near(k, h):
+        send_between(k, (h,), min(far_from, half_way) - 1, 1)
+        stat_to(k, h, z, oc)
 
     def wait_stats(k, h):
-        count = nblk * nrow - 1
+        count = (2 * reach + 1 if k == 0 else nblk) * nrow - 1
         copy = pltpu.make_async_remote_copy(
             stat_r.at[k, h, pl.ds(0, count)], stat_r.at[k, h, pl.ds(0, count)],
             stat_ssem.at[k, h], stat_rsem.at[k, h], device_id={"rows": oc}, device_id_type=MESH,
@@ -172,23 +206,54 @@
         copy.wait_send()
         copy.wait_recv()
 
+    def offset_of_row():
+        return lax.rem(iota((nblk * nrow, LANES), 0) // nrow + nblk - z, nblk)
+
+    def relay_copies(h, cores):
+        copies = []
+        for side, zz in enumerate((at(-reach), at(reach))):
+            for i, cc in enumerate(cores):
+                copies.append(pltpu.make_async_remote_copy(
+                    relay_s.at[h, side, pl.ds(0, 1)], relay_r.at[h, side, pl.ds(0, 1)], relay_ssem.at[h, side, i], relay_rsem.at[h, side],
+                    device_id={"blk": zz, "rows": cc}, device_id_type=MESH))
+        return copies
+
+    def relay():
+        offset = offset_of_row()
+        for h in range(halves):
+            everything = stat_r[0, h]
+            for side, (low, high) in enumerate(((1, reach), (nblk - reach + 1, nblk - 1))):
+                inside = jnp.logical_and(offset >= low, offset <= high)
+                part = jnp.sum(jnp.where(inside, everything, 0.0), axis=0, keepdims=True)
+                relay_s[h, side] = jnp.broadcast_to(part, (8, LANES))
+        for h in range(halves):
+            for copy in relay_copies(h, (oc, c)):
+                copy.start()
+
+    def relay_wait(h):
+        for copy in relay_copies(h, (oc,)):
+            copy.wait_recv()
+
     def scales(k, h, channels, gain, shift):
         count = pixels * nblk * nrow * (channels // GROUPS)
-        total = jnp.sum(stat_r[k, h], axis=0, keepdims=True) / count
-        total = jnp.broadcast_to(total, (16, LANES))
-        center = pltpu.roll(total, GROUPS, 1)
-        spread = lax.rsqrt(jnp.maximum(total - center * center, 0.0) + EPS)
-        slot_of_lane = iota((16, LANES), 1) // GROUPS
-        stat = jnp.where(slot_of_lane % 2 == 1, spread, total)
+        everything = stat_r[k, h]
+        if k == 0:
+            offset = offset_of_row()
+            inside = jnp.logical_or(offset <= reach, offset >= nblk - reach)
+            everything = jnp.where(inside, everything, 0.0)
+        total = jnp.sum(everything, axis=0, keepdims=True)
+        if k == 0:
+            total = total + relay_r[h, 0, 0:1] + relay_r[h, 1, 0:1]
         row = iota((16, LANES), 0)
-        stat = jnp.where(slot_of_lane == row % slots, stat, 0.0)
+        stat = jnp.where(iota((16, LANES), 1) // GROUPS == row % slots, total * (1.0 / count), 0.0)
         lhs = three_parts(stat, row // slots)
-        dots = jnp.dot(lhs, spread_matrix(channels), preferred_element_type=F32)
+        dots = jnp.dot(lhs, (spread1 if k == 0 else spread2)[...], preferred_element_type=F32)
         pick = lambda j: dots[j : j + 1] + dots[slots + j : slots + j + 1] + dots[2 * slots + j : 2 * slots + j + 1]
         result = []
         for i in range(per):
-            a = pick(2 * i + 1) * gain
-            result.append((0.5 * a, 0.5 * (shift - pick(2 * i) * a)))
+            center = pick(2 * i)
+            a = lax.rsqrt(jnp.maximum(pick(2 * i + 1) - center * center, 0.0) + EPS) * gain
+            result.append((0.5 * a, 0.5 * (shift - center * a)))
         return result
 
     def activate(values, ab):
@@ -243,20 +308,23 @@
             for i in range(per):
                 o.cor_s[h, side, pl.ds(i, 1)] = corners[i]
 
-    def emit(k, h, rows):
-        local_stats(k, h, rows)
-        send_stats(k, h)
-        prepare_halo(k, h)
+    def finish_sends(k, h):
+        send_near(k, h)
         for copy in halo_copies(k, h):
             copy.start()
+
+    def await_all(k, h):
+        if k == 0:
+            relay_wait(h)
+        else:
+            wait_stats(k, h)
+        for copy in halo_copies(k, h):
+            copy.wait()
 
     def load(k, h, a, gain, shift):
         o = halo_of(k)
         channels = o.channels
-        wait_stats(k, h)
         factors = scales(k, h, channels, gain, shift)
-        for copy in halo_copies(k, h):
-            copy.wait()
         column = iota((width, channels), 0)
 
         def put(image, row, act, low, high):
@@ -288,38 +356,52 @@
     def sums(values):
         return [jnp.sum(values, axis=0, keepdims=True), jnp.sum(values * values, axis=0, keepdims=True)]
 
-    for h in range(halves):
-        for i in range(per):
-            x_copies[h * per + i].wait()
+    for copy in x_copies:
+        copy.wait()
     rows0 = []
     for image in range(images):
         values = xv[image].reshape(pixels, xv.shape[-1]).astype(F32)
         v0[image] = values
         rows0.append(sums(values))
-    pl.semaphore_wait(barrier, nblk * nrow - 1)
     for h in range(halves):
-        emit(0, h, sum(rows0[h * per : (h + 1) * per], []))
-
+        local_stats(0, h, sum(rows0[h * per : (h + 1) * per], []))
+        prepare_halo(0, h)
+    pl.semaphore_wait(barrier, (2 * reach + 1) * nrow - 1)
+    send_between(0, range(halves), reach, 1)
+    for h in range(halves):
+        stat_to(0, h, z, oc)
+        for copy in halo_copies(0, h):
+            copy.start()
+
+    for copy in p_copies:
+        copy.wait()
     w_copies[0].wait()
     for image in range(images):
         stream[image] = jnp.dot(
             xv[image].reshape(pixels, xv.shape[-1]), sw[...], preferred_element_type=F32) + short_bias[...]
 
+    for h in range(halves):
+        wait_stats(0, h)
+
+    @pl.when(c == nrow - 1)
+    def _():
+        relay()
+
     last = 2 * RESNETS - 1
     for k in range(2 * RESNETS):
         if k == 0:
-            a, gain, shift, weight, bias = a1, gain_in[...], shift_in[...], w1, bias_first[...]
+            a, gain, shift, weight, bias = a1, gain_in, shift_in, w1, bias_first
         else:
-            j = k - 1
-            a, gain, shift, weight, bias = a2, gains[j : j + 1], shifts[j : j + 1], wr.at[j], biases[j : j + 1]
+            j = pl.ds(k - 1, 1)
+            a, gain, shift, weight, bias = a2, gains.at[j], shifts.at[j], wr.at[k - 1], biases.at[j]
+        w_copies[1 + k].wait()
         for h in range(halves):
-            load(k, h, a, gain, shift)
-            if h == 0:
-                w_copies[1 + k].wait()
+            await_all(k, h)
+            load(k, h, a, gain[...], shift[...])
             rows = []
             for i in range(per):
                 image = h * per + i
-                result = convolve(a, image, weight) + bias
+                result = convolve(a, image, weight) + bias[...]
                 if k % 2 == 1:
                     result = result + stream[image]
                 rounded = result.astype(BF16)
@@ -332,13 +414,18 @@
                         stream[image] = values
                     rows += sums(values)
             if k < last:
-                emit(k + 1, h, rows)
-            else:
-                pltpu.make_async_copy(
-                    outv.at[pl.ds(h * per, per)], out_hbm.at[pl.ds(h * per, per)], out_sem.at[h]).start()
-    for h in range(halves):
-        pltpu.make_async_copy(
-            outv.at[pl.ds(h * per, per)], out_hbm.at[pl.ds(h * per, per)], out_sem.at[h]).wait()
+                local_stats(k + 1, h, rows)
+                send_far(k + 1, h)
+                prepare_halo(k + 1, h)
+        if k < last:
+            for h in range(halves):
+                finish_sends(k + 1, h)
+
+    @pl.when(c == nrow - 1)
+    def _():
+        for h in range(halves):
+            for copy in relay_copies(h, (oc, c)):
+                copy.wait_send()
 
 
 def run(nblk, nrow, halves, *args):
@@ -350,7 +437,7 @@
     stages = 2 * RESNETS
     anywhere = pl.BlockSpec(memory_space=pl.ANY)
     inside = pl.BlockSpec(memory_space=pltpu.VMEM)
-    specs = [anywhere, inside, inside, anywhere, inside, anywhere, inside, inside, inside, anywhere, inside]
+    specs = [anywhere] * len(args)
     fixed = list(args)
     for j in (1, 2, 4, 6):
         fixed[j] = args[j].reshape(1, -1)
@@ -366,10 +453,15 @@
 
     return pl.pallas_call(
         functools.partial(kernel, nblk, nrow, halves),
-        out_shape=jax.ShapeDtypeStruct((images, height, width, ch), BF16),
+        out_shape=pltpu.VMEM((images, height, width, ch), BF16),
         in_specs=specs,
-        out_specs=anywhere,
+        out_specs=inside,
         scratch_shapes=[
+            *[pltpu.VMEM(fixed[j].shape, F32) for j in (1, 2, 4, 6, 7, 8, 10)],
+            pltpu.VMEM((cin, LANES), BF16),
+            pltpu.VMEM((ch, LANES), BF16),
+            pltpu.VMEM((LANES, cin), BF16),
+            pltpu.VMEM((LANES, ch), BF16),
             pltpu.VMEM(x.shape, BF16),
             pltpu.VMEM(w1.shape, BF16),
             pltpu.VMEM(wr.shape, BF16),
@@ -379,14 +471,17 @@
             pltpu.VMEM((images, height * width, ch), F32),
             pltpu.VMEM((images, height + 2, width, 3 * cin), BF16),
             pltpu.VMEM((images, height + 2, width, 3 * ch), BF16),
-            pltpu.VMEM((images, height, width, ch), BF16),
             *halo_buffers((), cin),
             *halo_buffers((stages - 1,), ch),
             pltpu.VMEM((stages, halves, 8, LANES), F32),
             pltpu.VMEM((stages, halves, nblk * nrow, LANES), F32),
+            pltpu.VMEM((halves, 2, 8, LANES), F32),
+            pltpu.VMEM((halves, 2, 8, LANES), F32),
             pltpu.SemaphoreType.DMA((images,)),
             pltpu.SemaphoreType.DMA((1 + stages,)),
-            pltpu.SemaphoreType.DMA((halves,)),
+            pltpu.SemaphoreType.DMA((7,)),
+            pltpu.SemaphoreType.DMA((halves, 2, 2)),
+            pltpu.SemaphoreType.DMA((halves, 2)),
             pltpu.SemaphoreType.DMA((stages, halves)),
             pltpu.SemaphoreType.DMA((stages, halves)),
             pltpu.SemaphoreType.DMA((stages, halves, 5)),

time: 121 us -> 112 us (0.926)
  Pallas kernels: 119 us -> 111 us
    pallas_call x1, Pallas kernels: 119 us -> 111 us  [run(): pl.pallas_call(functools.partial(kernel, nblk, nrow, halves), out_shape=p...]
where the time goes in v1:
time: 112 us
  Pallas kernels  111 us (99%)
    pallas_call x1, Pallas kernels, run(): pl.pallas_call(functools.partial(kernel, nblk, nrow, halves), out_shape=p...  111 us

profile of v1, /device:TPU:37, one launch (start us, length us, event | category | flops | bytes accessed | tf_op | source)
XLA Modules:
  0.0 112.1 jit_solution(16645074846905938612)
XLA Ops:
  0.0 111.3 %shard_map.109 = bf16[4,8,32,256]{3,2,1,0:T(8,128)(2,1)S(1)} custom-call(bf16[4,8,32,512]{3,2,1,0:T(8,128)(2,1)} %x_hbm.1, f32[1,512]{1,0:T(1,128)} %bitcast.4, f32[1,512]{1,0:T(1,128)} %bitcast.5, bf16[3,3,512,256]{3,2,1,0:T(8,128)(2,1)} %w1_hbm.1, f32[1,256]{1,0:T(1,128)} %bitcast.6, bf16[512,256]{1,0:T(8,128)(2,1)} %sw_hbm.1, f32[1,256]{1,0:T(1,128)} %bitcast.7, ...), custom_call_target="tpu_custom_call" | custom-call | tf_op jit(solution)/shard_map/pallas_call | solution.py:454
  111.3 0.8 copy.13

commit v2 on v1

--- a/solution.py
+++ b/solution.py
@@ -11,6 +11,7 @@
 RESNETS = 3
 EPS = 1e-06
 LANES = 128
+TAPS = (1, 0, 2)
 MESH = pl.DeviceIdType.MESH
 F32 = jnp.float32
 BF16 = jnp.bfloat16
@@ -72,7 +73,9 @@
     sw,
     v0,
     vs,
-    stream,
+    short,
+    s1,
+    s2,
     a1,
     a2,
     col_s1,
@@ -111,12 +114,15 @@
     right = lax.rem(z + 1, nblk)
     left = lax.rem(z + nblk - 1, nblk)
     me = z * nrow + c
-    edge = (height - 1) * (1 - c)
-    halo_row = (height + 1) * (1 - c)
-    zero_row = (height + 1) * c
+    edge = height - 1
+
+    def mirrored(row, rows):
+        return row + c * (rows - 1 - 2 * row)
+
 
     half_way = nblk // 2
-    reach = half_way // 2
+    reach = -(-half_way // 3)
+    leap = half_way - reach
     far_from = 2 * half_way // 3 + 1
 
     def at(offset):
@@ -134,11 +140,19 @@
     lax.fori_loop(0, reach, greet, 0)
     pl.semaphore_signal(barrier, 1, device_id={"rows": oc}, device_id_type=MESH)
 
-    x_copies = [pltpu.make_async_copy(x_hbm.at[i], xv.at[i], x_sem.at[i]) for i in range(images)]
-    w_copies = [
-        pltpu.make_async_copy(sw_hbm, sw, w_sem.at[0]),
-        pltpu.make_async_copy(w1_hbm, w1, w_sem.at[1]),
-    ] + [pltpu.make_async_copy(wr_hbm.at[i], wr.at[i], w_sem.at[2 + i]) for i in range(wr_hbm.shape[0])]
+    x_waits = [pltpu.make_async_copy(x_hbm.at[i], xv.at[i], x_sem.at[i]) for i in range(images)]
+    x_copies = [
+        pltpu.make_async_copy(x_hbm.at[i, mirrored(r, height)], xv.at[i, r], x_sem.at[i])
+        for i in range(images) for r in range(height)
+    ]
+    kernels = [(w1_hbm, w1)] + [(wr_hbm.at[i], wr.at[i]) for i in range(wr_hbm.shape[0])]
+    w_waits = [pltpu.make_async_copy(sw_hbm, sw, w_sem.at[0])]
+    w_copies = [w_waits[0]]
+    for i, (source, target) in enumerate(kernels):
+        w_waits.append(pltpu.make_async_copy(source, target, w_sem.at[1 + i]))
+        for slot, tap in enumerate(TAPS):
+            for d in range(3):
+                w_copies.append(pltpu.make_async_copy(source.at[mirrored(d, 3), tap], target.at[d, slot], w_sem.at[1 + i]))
     p_copies = [
         pltpu.make_async_copy(source, target, p_sem.at[i])
         for i, (source, target) in enumerate((
@@ -154,7 +168,7 @@
     spread2[...] = spread_matrix(spread2.shape[1])
     for a in (a1, a2):
         for i in range(images):
-            a[i, zero_row] = jnp.zeros(a.shape[2:], BF16)
+            a[i, 0] = jnp.zeros(a.shape[2:], BF16)
 
     def local_stats(k, h, rows):
         channels = rows[0].shape[1]
@@ -168,7 +182,6 @@
         slot_of_lane = iota((16, LANES), 1) // GROUPS
         packed = jnp.sum(jnp.where(slot_of_row == slot_of_lane, dots, 0.0), axis=0, keepdims=True)
         stat_s[k, h] = jnp.broadcast_to(packed, (8, LANES))
-        stat_r[k, h, pl.ds(me, 1)] = packed
 
     def stat_to(k, h, zz, cc):
         pltpu.make_async_remote_copy(
@@ -194,7 +207,7 @@
         send_between(k, (h,), half_way - 1, far_from)
 
     def send_near(k, h):
-        send_between(k, (h,), min(far_from, half_way) - 1, 1)
+        send_between(k, (h,), far_from - 1, 1)
         stat_to(k, h, z, oc)
 
     def wait_stats(k, h):
@@ -206,12 +219,17 @@
         copy.wait_send()
         copy.wait_recv()
 
-    def offset_of_row():
-        return lax.rem(iota((nblk * nrow, LANES), 0) // nrow + nblk - z, nblk)
+    def gathered(k, h):
+        own = iota((nblk * nrow, LANES), 0) == me
+        return jnp.where(own, stat_s[k, h, 0:1], stat_r[k, h])
+
+    def between(low, high):
+        chip = iota((nblk * nrow, LANES), 0) // nrow
+        return lax.rem(chip + 2 * nblk - z - low, nblk) <= high - low
 
     def relay_copies(h, cores):
         copies = []
-        for side, zz in enumerate((at(-reach), at(reach))):
+        for side, zz in enumerate((at(-leap), at(leap))):
             for i, cc in enumerate(cores):
                 copies.append(pltpu.make_async_remote_copy(
                     relay_s.at[h, side, pl.ds(0, 1)], relay_r.at[h, side, pl.ds(0, 1)], relay_ssem.at[h, side, i], relay_rsem.at[h, side],
@@ -219,12 +237,10 @@
         return copies
 
     def relay():
-        offset = offset_of_row()
         for h in range(halves):
-            everything = stat_r[0, h]
-            for side, (low, high) in enumerate(((1, reach), (nblk - reach + 1, nblk - 1))):
-                inside = jnp.logical_and(offset >= low, offset <= high)
-                part = jnp.sum(jnp.where(inside, everything, 0.0), axis=0, keepdims=True)
+            everything = gathered(0, h)
+            for side, (low, high) in enumerate(((reach + 1 - leap, reach), (1 - reach, leap - reach - 1))):
+                part = jnp.sum(jnp.where(between(low, high), everything, 0.0), axis=0, keepdims=True)
                 relay_s[h, side] = jnp.broadcast_to(part, (8, LANES))
         for h in range(halves):
             for copy in relay_copies(h, (oc, c)):
@@ -236,11 +252,9 @@
 
     def scales(k, h, channels, gain, shift):
         count = pixels * nblk * nrow * (channels // GROUPS)
-        everything = stat_r[k, h]
+        everything = gathered(k, h)
         if k == 0:
-            offset = offset_of_row()
-            inside = jnp.logical_or(offset <= reach, offset >= nblk - reach)
-            everything = jnp.where(inside, everything, 0.0)
+            everything = jnp.where(between(-reach, reach), everything, 0.0)
         total = jnp.sum(everything, axis=0, keepdims=True)
         if k == 0:
             total = total + relay_r[h, 0, 0:1] + relay_r[h, 1, 0:1]
@@ -272,7 +286,8 @@
         o.row_r = row_r1 if first else row_r2.at[k - 1]
         o.cor_s = cor_s1 if first else cor_s2.at[k - 1]
         o.cor_r = cor_r1 if first else cor_r2.at[k - 1]
-        o.channels = o.v.shape[-1]
+        o.tiles = o.v.shape[1]
+        o.channels = o.tiles * LANES
         return o
 
     def halo_copies(k, h):
@@ -283,10 +298,10 @@
                 o.col_s.at[h, side], o.col_r.at[h, side], halo_ssem.at[k, h, 2 * side], colr_sem.at[k, h, side],
                 device_id={"blk": blk, "rows": c}, device_id_type=MESH))
             copies.append(pltpu.make_async_remote_copy(
-                o.cor_s.at[h, side], o.cor_r.at[h, side], halo_ssem.at[k, h, 2 * side + 1], corr_sem.at[k, h, side],
+                o.cor_s.at[h, side, pl.ds(0, per)], o.cor_r.at[h, side, pl.ds(0, per)], halo_ssem.at[k, h, 2 * side + 1], corr_sem.at[k, h, side],
                 device_id={"blk": blk, "rows": oc}, device_id_type=MESH))
         copies.append(pltpu.make_async_remote_copy(
-            o.v.at[pl.ds(h * per, per), pl.ds(edge * width, width)], o.row_r.at[h], halo_ssem.at[k, h, 4], rowr_sem.at[k, h],
+            o.v.at[pl.ds(h * per, per), :, pl.ds(edge * width, width)], o.row_r.at[h], halo_ssem.at[k, h, 4], rowr_sem.at[k, h],
             device_id={"rows": oc}, device_id_type=MESH))
         return copies
 
@@ -294,19 +309,12 @@
         o = halo_of(k)
         for side in range(2):
             q = width - 1 if side == 0 else 0
-            cols = []
-            corners = []
-            for i in range(per):
-                image = h * per + i
-                which = iota((height, o.channels), 0)
-                col = jnp.broadcast_to(o.v[image, pl.ds(q, 1), :], (height, o.channels))
-                for r in range(1, height):
-                    col = jnp.where(which == r, o.v[image, pl.ds(r * width + q, 1), :], col)
-                cols.append(col)
-                corners.append(o.v[image, pl.ds(edge * width + q, 1), :])
-            o.col_s[h, side] = jnp.concatenate(cols, axis=0).astype(BF16)
-            for i in range(per):
-                o.cor_s[h, side, pl.ds(i, 1)] = corners[i]
+            for t in range(o.tiles):
+                lanes = pl.ds(t * LANES, LANES)
+                cols = [o.v[h * per + i, t, pl.ds(q, height, stride=width), :] for i in range(per)]
+                o.col_s[h, side, :, lanes] = jnp.concatenate(cols, axis=0).astype(BF16)
+                for i in range(per):
+                    o.cor_s[h, side, pl.ds(i, 1), lanes] = o.v[h * per + i, t, pl.ds(edge * width + q, 1), :]
 
     def finish_sends(k, h):
         send_near(k, h)
@@ -314,54 +322,66 @@
             copy.start()
 
     def await_all(k, h):
+        for copy in halo_copies(k, h):
+            copy.wait()
         if k == 0:
             relay_wait(h)
         else:
             wait_stats(k, h)
-        for copy in halo_copies(k, h):
-            copy.wait()
 
     def load(k, h, a, gain, shift):
         o = halo_of(k)
         channels = o.channels
         factors = scales(k, h, channels, gain, shift)
-        column = iota((width, channels), 0)
-
-        def put(image, row, act, low, high):
-            a[image, row, :, pl.ds(0, channels)] = jnp.where(column == 0, low, pltpu.roll(act, 1, 0)).astype(BF16)
-            a[image, row, :, pl.ds(channels, channels)] = act.astype(BF16)
-            a[image, row, :, pl.ds(2 * channels, channels)] = jnp.where(
-                column == width - 1, high, pltpu.roll(act, width - 1, 0)).astype(BF16)
-
+        pitch = width + 16
         for i in range(per):
             image = h * per + i
-            ab = factors[i]
-            sides = [activate(o.col_r[h, s, pl.ds(i * height, height)].astype(F32), ab) for s in range(2)]
-            corner = [activate(o.cor_r[h, s, pl.ds(i, 1)], ab) for s in range(2)]
-            for r in range(height):
-                act = activate(o.v[image, pl.ds(r * width, width), :], ab)
-                put(image, r + 1, act, sides[0][r : r + 1], sides[1][r : r + 1])
-            act = activate(o.row_r[h, i], ab)
-            put(image, halo_row, act, corner[0], corner[1])
+            shelf = s1.at[image] if k == 0 else s2.at[i]
+            tiles = [slice(t * LANES, (t + 1) * LANES) for t in range(o.tiles)]
+            ab = [[x[:, t] for x in factors[i]] for t in tiles]
+
+            for s, at_column in enumerate((7, width + 8)):
+                for t, lanes in enumerate(tiles):
+                    side = activate(o.col_r[h, s, pl.ds(i * height, height), lanes].astype(F32), ab[t])
+                    shelf[t, pl.ds(at_column, height, stride=pitch), :] = side
+                    shelf[t, pl.ds(height * pitch + at_column, 1), :] = activate(o.cor_r[h, s, pl.ds(i, 1), lanes], ab[t])
+            for r in range(height + 1):
+                center = []
+                for t in range(o.tiles):
+                    source = o.v[image, t, pl.ds(r * width, width), :] if r < height else o.row_r[h, i, t]
+                    act = activate(source, ab[t])
+                    shelf[t, pl.ds(r * pitch + 8, width), :] = act
+                    center.append(act)
+                a[image, r + 1, :, pl.ds(0, channels)] = jnp.concatenate(center, axis=1).astype(BF16)
+            for slot in (1, 2):
+                for r in range(height + 1):
+                    moved = [shelf[t, pl.ds(r * pitch + 7 + TAPS[slot], width), :] for t in range(o.tiles)]
+                    a[image, r + 1, :, pl.ds(slot * channels, channels)] = jnp.concatenate(moved, axis=1).astype(BF16)
 
     def convolve(a, image, weight):
         depth = a.shape[-1]
         total = None
-        for d in range(3):
-            lhs = a[image, d : d + height].reshape(pixels, depth)
-            term = jnp.dot(lhs, weight[d].reshape(depth, weight.shape[-1]), preferred_element_type=F32)
-            total = term if total is None else total + term
+        step = depth // 3
+        for slot in range(3):
+            for d in TAPS:
+                lhs = a[image, d : d + height, :, pl.ds(slot * step, step)].reshape(pixels, step)
+                term = jnp.dot(lhs, weight[d, slot], preferred_element_type=F32)
+                total = term if total is None else total + term
         return total
+
+    def put(target, values):
+        for t in range(target.shape[0]):
+            target[t] = values[:, t * LANES : (t + 1) * LANES]
 
     def sums(values):
         return [jnp.sum(values, axis=0, keepdims=True), jnp.sum(values * values, axis=0, keepdims=True)]
 
-    for copy in x_copies:
+    for copy in x_waits:
         copy.wait()
     rows0 = []
     for image in range(images):
         values = xv[image].reshape(pixels, xv.shape[-1]).astype(F32)
-        v0[image] = values
+        put(v0.at[image], values)
         rows0.append(sums(values))
     for h in range(halves):
         local_stats(0, h, sum(rows0[h * per : (h + 1) * per], []))
@@ -375,10 +395,10 @@
 
     for copy in p_copies:
         copy.wait()
-    w_copies[0].wait()
+    w_waits[0].wait()
     for image in range(images):
-        stream[image] = jnp.dot(
-            xv[image].reshape(pixels, xv.shape[-1]), sw[...], preferred_element_type=F32) + short_bias[...]
+        put(short.at[image], jnp.dot(
+            xv[image].reshape(pixels, xv.shape[-1]), sw[...], preferred_element_type=F32) + short_bias[...])
 
     for h in range(halves):
         wait_stats(0, h)
@@ -394,24 +414,30 @@
         else:
             j = pl.ds(k - 1, 1)
             a, gain, shift, weight, bias = a2, gains.at[j], shifts.at[j], wr.at[k - 1], biases.at[j]
-        w_copies[1 + k].wait()
+        w_waits[1 + k].wait()
         for h in range(halves):
-            await_all(k, h)
-            load(k, h, a, gain[...], shift[...])
+            if k > 0:
+                await_all(k, h)
+                load(k, h, a, gain[...], shift[...])
+            elif h == 0:
+                for g in range(halves):
+                    await_all(k, g)
+                for g in range(halves):
+                    load(k, g, a, gain[...], shift[...])
             rows = []
             for i in range(per):
                 image = h * per + i
                 result = convolve(a, image, weight) + bias[...]
                 if k % 2 == 1:
-                    result = result + stream[image]
+                    skip = short.at[image] if k == 1 else vs.at[k - 2, image]
+                    result = result + jnp.concatenate([skip[t] for t in range(skip.shape[0])], axis=1)
                 rounded = result.astype(BF16)
                 if k == last:
-                    outv[image] = rounded.reshape(height, width, rounded.shape[-1])
+                    for r in range(height):
+                        outv[image, mirrored(r, height)] = rounded[r * width : (r + 1) * width]
                 else:
                     values = rounded.astype(F32)
-                    vs[k, image] = values
-                    if k % 2 == 1:
-                        stream[image] = values
+                    put(vs.at[k, image], values)
                     rows += sums(values)
             if k < last:
                 local_stats(k + 1, h, rows)
@@ -446,7 +472,7 @@
         return [
             pltpu.VMEM((*lead, halves, 2, per * height, channels), BF16),
             pltpu.VMEM((*lead, halves, 2, per * height, channels), BF16),
-            pltpu.VMEM((*lead, halves, per, width, channels), F32),
+            pltpu.VMEM((*lead, halves, per, channels // LANES, width, LANES), F32),
             pltpu.VMEM((*lead, halves, 2, 8, channels), F32),
             pltpu.VMEM((*lead, halves, 2, 8, channels), F32),
         ]
@@ -466,9 +492,11 @@
             pltpu.VMEM(w1.shape, BF16),
             pltpu.VMEM(wr.shape, BF16),
             pltpu.VMEM((cin, ch), BF16),
-            pltpu.VMEM((images, height * width, cin), F32),
-            pltpu.VMEM((stages - 1, images, height * width, ch), F32),
-            pltpu.VMEM((images, height * width, ch), F32),
+            pltpu.VMEM((images, cin // LANES, height * width, LANES), F32),
+            pltpu.VMEM((stages - 1, images, ch // LANES, height * width, LANES), F32),
+            pltpu.VMEM((images, ch // LANES, height * width, LANES), F32),
+            pltpu.VMEM((images, cin // LANES, (height + 1) * (width + 16), LANES), F32),
+            pltpu.VMEM((per, ch // LANES, (height + 1) * (width + 16), LANES), F32),
             pltpu.VMEM((images, height + 2, width, 3 * cin), BF16),
             pltpu.VMEM((images, height + 2, width, 3 * ch), BF16),
             *halo_buffers((), cin),

time: 112 us -> 112 us (level)
  no operation moved by 1% of the time
where the time goes in v2:
time: 112 us; the launch traced here: 111 us
  Pallas kernels  111 us (99%)
    pallas_call x1, Pallas kernels, run(): pl.pallas_call(functools.partial(kernel, nblk, nrow, halves), out_shape=p...  111 us

profile of v2, /device:TPU:37, one launch (start us, length us, event | category | flops | bytes accessed | tf_op | source)
XLA Modules:
  0.0 111.4 jit_solution(4743951722197513281)
XLA Ops:
  0.0 110.6 %shard_map.109 = bf16[4,8,32,256]{3,2,1,0:T(8,128)(2,1)S(1)} custom-call(bf16[4,8,32,512]{3,2,1,0:T(8,128)(2,1)} %x_hbm.1, f32[1,512]{1,0:T(1,128)} %bitcast.4, f32[1,512]{1,0:T(1,128)} %bitcast.5, bf16[3,3,512,256]{3,2,1,0:T(8,128)(2,1)} %w1_hbm.1, f32[1,256]{1,0:T(1,128)} %bitcast.6, bf16[512,256]{1,0:T(8,128)(2,1)} %sw_hbm.1, f32[1,256]{1,0:T(1,128)} %bitcast.7, ...), custom_call_target="tpu_custom_call" | custom-call | tf_op jit(solution)/shard_map/pallas_call | solution.py:480
  110.6 0.8 copy.13
